TPU v7x, 256 devices: a whole 4x4x8 slice. The times are simulated.
256 devices in a mesh: ent: 128 (over x, y, z_lo, core), grp: 2 (over z_hi).
Axes of the slice: x: 4, y: 4, z: 8 (z_hi: 2, z_lo: 4; z = z_hi * 4 + z_lo), core: 2. Of those that a mesh axis runs over, the one named last changes fastest.
Arguments:
- entity_table: bfloat16 [65536, 1024], P('ent'), may hold values from -2.5 to 2.5
- rel_phases: float32 [822, 512], replicated, may hold values from -3.1416 to 3.1416
- head_ids: int32 [65536], P(('ent', 'grp')), may hold values from 0 to 511
- rel_ids: int32 [65536], P(('ent', 'grp')), may hold values from 0 to 821
- target_pos: int32 [65536], P(('ent', 'grp')), may hold values from 0 to 511
- block_owner: int32 [4], replicated, may hold values from 0 to 127
- block_local: int32 [4], replicated, may hold values from 0 to 3
Outputs:
- losses: float32 [65536], P(('ent', 'grp'))
- head_grad: bfloat16 [65536, 1024], P(('ent', 'grp'))
- table_grad: bfloat16 [65536, 1024], P('ent')
- rel_grad: float32 [822, 512], replicated
Inputs may be any that keep to these rules, and one draw needn't show every extreme that they name: query q on device d (ent then grp) has head row (d // 2) * 512 + head_ids[q]. `target_pos`: position among the 512 candidates, block after block. Block b covers table rows from (block_owner[b] * 4 + block_local[b]) * 128 on; blocks may repeat.
All inputs are finite; a program needn't handle non-finite values.
Results may differ from a plain program's by a relative error of at most 0.0057.
Values may be sent and summed in bfloat16 or wider, within the bound.
A program may use at most 64 MiB of HBM per device.

v0:
```python
import jax
import jax.numpy as jnp
from jax import lax
from jax.sharding import Mesh
from jax.sharding import PartitionSpec as P

BLK = 128
ENT = ("ent_0", "ent_1", "ent_2", "ent_3")
ENT_GRP = ("ent_0", "ent_1", "ent_2", "ent_3", "grp")


SOFTMAX_TEMPER = 2.0


def broadcast_by_axis(value, axes, root):
    value = jnp.where(lax.axis_index(axes) == root, value, jnp.zeros_like(value))
    for axis in axes:
        value = lax.psum(value, axis)
    return value


def joined_along(parts, dim):
    parts = jnp.moveaxis(parts, 0, dim)
    dims = parts.shape
    return parts.reshape(*dims[:dim], dims[dim] * dims[dim + 1], *dims[dim + 2 :])


def copy_for_each(value, axis):
    copies = jnp.broadcast_to(value, (lax.axis_size(axis), *value.shape))
    return lax.all_to_all(copies, axis, split_axis=0, concat_axis=0, tiled=True)


def gather_directly(value, axis, dim):
    return joined_along(copy_for_each(value, axis), dim)


def body(entity_table, rel_phases, head_ids, rel_ids, target_pos, block_owner, block_local):
    half_dim = rel_phases.shape[1]
    rel_count = rel_phases.shape[0]
    shard_rows = entity_table.shape[0]
    blocks_total = block_owner.shape[0]
    blank = jnp.zeros((blocks_total, BLK, 2 * half_dim), jnp.bfloat16)
    share = blocks_total // lax.axis_size("grp")
    offset = lax.axis_index("grp") * share

    def fetch_share(position, buffer):
        wanted = offset + position
        own_block = lax.dynamic_slice_in_dim(entity_table, block_local[wanted] * BLK, BLK, 0)
        arrived = broadcast_by_axis(own_block, ENT, block_owner[wanted])
        return lax.dynamic_update_slice_in_dim(buffer, arrived[None], position, 0)

    halves = lax.fori_loop(0, share, fetch_share, blank[:share])
    fetched = gather_directly(halves, "grp", 0)
    candidate_block = fetched.reshape(blocks_total * BLK, 2 * half_dim)
    heads = jnp.take(entity_table, head_ids, axis=0).astype(jnp.float32)
    angles = jnp.take(rel_phases, rel_ids, axis=0)
    cosine = jnp.cos(angles)
    sine = jnp.sin(angles)
    real_head = heads[:, :half_dim]
    imag_head = heads[:, half_dim:]
    real_query = real_head * cosine - imag_head * sine
    imag_query = real_head * sine + imag_head * cosine
    query_reduced_precision = jnp.concatenate([real_query, imag_query], axis=1).astype(jnp.bfloat16)
    candidate_norm = jnp.sum(jnp.square(candidate_block.astype(jnp.float32)), axis=1)
    inner_products = lax.dot_general(
        query_reduced_precision,
        candidate_block,
        (((1,), (1,)), ((), ())),
        preferred_element_type=jnp.float32,
    )
    logit_scores = (2.0 * inner_products - candidate_norm[None, :]) / SOFTMAX_TEMPER
    top = jnp.max(logit_scores, axis=1, keepdims=True)
    log_total = top[:, 0] + jnp.log(jnp.sum(jnp.exp(logit_scores - top), axis=1))
    picked = jnp.take_along_axis(logit_scores, target_pos[:, None], axis=1)[:, 0]
    losses = log_total - picked
    columns = jnp.arange(logit_scores.shape[1], dtype=jnp.int32)
    onehot = (columns[None, :] == target_pos[:, None]).astype(jnp.float32)
    softmax_weights = jnp.exp(logit_scores - log_total[:, None]) - onehot
    weights_reduced_precision = softmax_weights.astype(jnp.bfloat16)
    query_gradient = (
        2.0
        / SOFTMAX_TEMPER
        * jnp.dot(weights_reduced_precision, candidate_block, preferred_element_type=jnp.float32)
    )
    back_products = lax.dot_general(
        weights_reduced_precision,
        query_reduced_precision,
        (((0,), (0,)), ((), ())),
        preferred_element_type=jnp.float32,
    )
    candidate_gradient = (
        2.0
        / SOFTMAX_TEMPER
        * (
            back_products
            - jnp.sum(softmax_weights, axis=0)[:, None] * candidate_block.astype(jnp.float32)
        )
    )
    real_grad = query_gradient[:, :half_dim]
    imag_grad = query_gradient[:, half_dim:]
    head_grad = jnp.concatenate(
        [real_grad * cosine + imag_grad * sine, imag_grad * cosine - real_grad * sine], axis=1
    ).astype(jnp.bfloat16)
    angle_grad = imag_grad * real_query - real_grad * imag_query
    rel_part = jax.ops.segment_sum(angle_grad, rel_ids, num_segments=rel_count)
    summed, rel_grad = lax.psum((candidate_gradient, rel_part), ENT_GRP)
    block_numbers = jnp.arange(shard_rows // BLK, dtype=jnp.int32)
    selector = (
        (block_owner == lax.axis_index(ENT))[:, None]
        & (block_local[:, None] == block_numbers[None, :])
    ).astype(jnp.float32)
    placed = jnp.einsum(
        "jb,jrk->brk",
        selector,
        summed.reshape(blocks_total, BLK, 2 * half_dim),
        precision=lax.Precision.HIGHEST,
    )
    table_grad = placed.reshape(shard_rows, 2 * half_dim).astype(jnp.bfloat16)
    return (losses, head_grad, table_grad, rel_grad)


def solution(mesh):
    finer = Mesh(
        mesh.devices.reshape(4, 4, 4, 2, mesh.shape["grp"]),
        ("ent_0", "ent_1", "ent_2", "ent_3", "grp"),
    )
    placed = (P(ENT, None), P(), P(ENT_GRP), P(ENT_GRP), P(ENT_GRP), P(), P())
    return jax.shard_map(
        body,
        mesh=finer,
        in_specs=placed,
        out_specs=(P(ENT_GRP), P(ENT_GRP, None), P(ENT, None), P()),
        check_vma=False,
    )
```

profile of v0, /device:TPU:1, one launch (start us, length us, event | category | flops | bytes accessed | tf_op | source)
XLA Modules:
  0.0 717.7 jit_solution(12075199189034619199)
XLA Ops:
  8.0 379.1 %while.13 = (s32[]{:T(128)}, bf16[2,128,1024]{2,1,0:T(8,128)(2,1)S(1)}, s32[]{:T(128)}, s32[4]{0:T(128)}, s32[4]{0:T(128)}, /*index=5*/bf16[512,1024]{1,0:T(8,12...) while((s32[]{:T(128)}, ...), condition=%wide.region_5.6_spmd, body=%wide.region_0.5_spmd.sunk | while | flops 655389 | bytes 7340707 | solution.py:52
  8.0 0.0 all-reduce.9.cloned.1.call-start
  8.1 1.3 dynamic_slice.27
  9.5 1.2 dynamic_slice.26
  12.0 1.7 dynamic-slice_select_fusion.2
  13.7 0.0 all-reduce.11.cloned.1.call-start
  13.8 48.7 %all-reduce.9.cloned.1.call-done = bf16[128,1024]{1,0:T(8,128)(2,1)} async-done(((bf16[128,1024]{1,0:T(8,128)(2,1)}), bf16[128,1024]{1,0:T(8,128)(2,1)}) %all-reduce.9.cloned.1.call-update) | async-done | bytes 262160 | tf_op jit(solution)/shard_map/while/body/eval_jaxpr/psum | solution.py:18
  62.5 0.0 all-reduce.13.cloned.1.call-start
  62.6 49.8 %all-reduce.11.cloned.1.call-done = bf16[128,1024]{1,0:T(8,128)(2,1)} async-done(((bf16[128,1024]{1,0:T(8,128)(2,1)}), bf16[128,1024]{1,0:T(8,128)(2,1)}) %all-reduce.11.cloned.1.call-update) | async-done | bytes 262160 | tf_op jit(solution)/shard_map/while/body/eval_jaxpr/psum | solution.py:18
  112.4 0.0 all-reduce.15.cloned.1.call-start
  112.4 52.8 %all-reduce.13.cloned.1.call-done = bf16[128,1024]{1,0:T(8,128)(2,1)} async-done(((bf16[128,1024]{1,0:T(8,128)(2,1)}), bf16[128,1024]{1,0:T(8,128)(2,1)}) %all-reduce.13.cloned.1.call-update) | async-done | bytes 262160 | tf_op jit(solution)/shard_map/while/body/eval_jaxpr/psum | solution.py:18
  165.3 33.0 %all-reduce.15.cloned.1.call-done = bf16[1,128,1024]{2,1,0:T(8,128)(2,1)} async-done(((bf16[1,128,1024]{2,1,0:T(8,128)(2,1)}), bf16[1,128,1024]{2,1,0:T(8,128)(2,1)}) %all-reduce.15.cloned.1.call-update) | async-done | bytes 262160 | tf_op jit(solution)/shard_map/while/body/eval_jaxpr/psum | solution.py:18
  198.3 1.0 constant_dynamic-update-slice_fusion.2
  199.3 0.0 all-reduce.9.cloned.1.call-start
  199.3 1.2 dynamic_slice.27
  200.6 1.2 dynamic_slice.26
  203.1 1.7 dynamic-slice_select_fusion.2
  204.9 0.0 all-reduce.11.cloned.1.call-start
  204.9 45.5 %all-reduce.9.cloned.1.call-done = bf16[128,1024]{1,0:T(8,128)(2,1)} async-done(((bf16[128,1024]{1,0:T(8,128)(2,1)}), bf16[128,1024]{1,0:T(8,128)(2,1)}) %all-reduce.9.cloned.1.call-update) | async-done | bytes 262160 | tf_op jit(solution)/shard_map/while/body/eval_jaxpr/psum | solution.py:18
  250.5 49.6 %all-reduce.11.cloned.1.call-done = bf16[128,1024]{1,0:T(8,128)(2,1)} async-done(((bf16[128,1024]{1,0:T(8,128)(2,1)}), bf16[128,1024]{1,0:T(8,128)(2,1)}) %all-reduce.11.cloned.1.call-update) | async-done | bytes 262160 | tf_op jit(solution)/shard_map/while/body/eval_jaxpr/psum | solution.py:18
  300.2 52.8 %all-reduce.13.cloned.1.call-done = bf16[128,1024]{1,0:T(8,128)(2,1)} async-done(((bf16[128,1024]{1,0:T(8,128)(2,1)}), bf16[128,1024]{1,0:T(8,128)(2,1)}) %all-reduce.13.cloned.1.call-update) | async-done | bytes 262160 | tf_op jit(solution)/shard_map/while/body/eval_jaxpr/psum | solution.py:18
  353.0 33.1 %all-reduce.15.cloned.1.call-done = bf16[1,128,1024]{2,1,0:T(8,128)(2,1)} async-done(((bf16[1,128,1024]{2,1,0:T(8,128)(2,1)}), bf16[1,128,1024]{2,1,0:T(8,128)(2,1)}) %all-reduce.15.cloned.1.call-update) | async-done | bytes 262160 | tf_op jit(solution)/shard_map/while/body/eval_jaxpr/psum | solution.py:18
  386.2 1.0 constant_dynamic-update-slice_fusion.2
  387.2 1.1 broadcast_in_dim.60
  388.3 6.5 all-to-all-start
  394.9 1.2 gather_fusion
  396.1 1.0 gather_fusion.1
  397.1 0.1 select_convert_fusion
  397.2 3.2 fusion.25
  400.4 15.2 %all-to-all-done = bf16[2,2,128,1024]{3,2,1,0:T(8,128)(2,1)} async-done(((bf16[2,2,128,1024]{3,2,1,0:T(8,128)(2,1)}), bf16[2,2,128,1024]{3,2,1,0:T(8,128)(2,1)}, u32[]{:S(2)}, u32[]{:S(2)}) %all-to-all-start) | async-done | bytes 1048608 | tf_op jit(solution)/shard_map/all_to_all | solution.py:30
  415.6 1.5 multiply_reduce_fusion
  417.1 1.8 fusion.27
  418.9 2.3 gather_fusion.2
  421.3 0.2 exponential_reduce_fusion
  421.5 0.6 fusion.14
  422.1 0.2 fusion.9
  422.3 1.7 fusion.23
  424.1 1.8 multiply_subtract_fusion
  425.9 2.7 copy.12
  428.6 3.9 scatter_custom_fusion
  432.6 0.6 copy-done.12
  433.2 0.4 copy-done.3
  433.6 2.3 add_convert_fusion
  435.9 0.9 pad_maximum_fusion.1
  436.8 267.2 %all-reduce.7.cloned.1.call-done = (f32[4,128,1024]{2,0,1:T(4,128)}, f32[822,512]{1,0:T(8,128)}) async-done(((f32[4,128,1024]{2,0,1:T(4,128)}, f32[822,512]{1,0:T(8,128)}), (f32[4,128,1024]{2,0,1:T(4,128)}, f32[822,512]{1,0:T(8,128)})) %all-reduce.7.cloned.1.call-update) | async-done | bytes 3780624 | tf_op jit(solution)/shard_map/psum | solution.py:106
  704.0 3.8 convolution_convert_fusion
  707.8 1.3 copy.13
  709.1 1.2 copy.27
  (48 shorter events, 0.4 us)
Async XLA Ops:
  8.0 388.1 %copy-start = (f32[822,512]{1,0:T(8,128)S(1)}, f32[822,512]{1,0:T(8,128)}, u32[]{:S(2)}) copy-start(f32[822,512]{1,0:T(8,128)} %param.10) | copy-start | bytes 5050372
  8.0 54.5 %all-reduce.9.cloned.1.call-start = ((), (), s32[]{:S(2)}) async-start(), calls=%async_computation.2 | async-start | bytes 524288 | tf_op jit(solution)/shard_map/while/body/eval_jaxpr/psum | solution.py:18
  13.7 98.6 %all-reduce.11.cloned.1.call-start = ((), (), s32[]{:S(2)}) async-start(), calls=%async_computation.3 | async-start | bytes 524288 | tf_op jit(solution)/shard_map/while/body/eval_jaxpr/psum | solution.py:18
  62.5 102.7 %all-reduce.13.cloned.1.call-start = ((), (), s32[]{:S(2)}) async-start(), calls=%async_computation.4 | async-start | bytes 524288 | tf_op jit(solution)/shard_map/while/body/eval_jaxpr/psum | solution.py:18
  112.4 85.9 %all-reduce.15.cloned.1.call-start = ((), (), s32[]{:S(2)}) async-start(), calls=%async_computation.5 | async-start | bytes 524288 | tf_op jit(solution)/shard_map/while/body/eval_jaxpr/psum | solution.py:18
  199.3 51.1 %all-reduce.9.cloned.1.call-start = ((), (), s32[]{:S(2)}) async-start(), calls=%async_computation.2 | async-start | bytes 524288 | tf_op jit(solution)/shard_map/while/body/eval_jaxpr/psum | solution.py:18
  204.9 95.3 %all-reduce.11.cloned.1.call-start = ((), (), s32[]{:S(2)}) async-start(), calls=%async_computation.3 | async-start | bytes 524288 | tf_op jit(solution)/shard_map/while/body/eval_jaxpr/psum | solution.py:18
  250.4 102.6 %all-reduce.13.cloned.1.call-start = ((), (), s32[]{:S(2)}) async-start(), calls=%async_computation.4 | async-start | bytes 524288 | tf_op jit(solution)/shard_map/while/body/eval_jaxpr/psum | solution.py:18
  300.2 86.0 %all-reduce.15.cloned.1.call-start = ((), (), s32[]{:S(2)}) async-start(), calls=%async_computation.5 | async-start | bytes 524288 | tf_op jit(solution)/shard_map/while/body/eval_jaxpr/psum | solution.py:18
  387.2 7.6 %copy-start.10 = (s32[256]{0:T(256)S(1)}, s32[256]{0:T(256)}, u32[]{:S(2)}) copy-start(s32[256]{0:T(256)} %param.12) | copy-start | bytes 3076
  387.2 7.6 %copy-start.9 = (s32[256]{0:T(256)S(1)}, s32[256]{0:T(256)}, u32[]{:S(2)}) copy-start(s32[256]{0:T(256)} %param.11) | copy-start | bytes 3076
  387.2 7.6 %copy-start.8 = (s32[256]{0:T(256)S(1)}, s32[256]{0:T(256)}, u32[]{:S(2)}) copy-start(s32[256]{0:T(256)} %param.13) | copy-start | bytes 3076
  387.2 7.7 %copy-start.1 = (bf16[512,1024]{1,0:T(8,128)(2,1)S(1)}, bf16[512,1024]{1,0:T(8,128)(2,1)}, u32[]{:S(2)}) copy-start(bf16[512,1024]{1,0:T(8,128)(2,1)} %get-tuple-element.246) | copy-start | bytes 3145732
  388.3 27.3 %all-to-all-start = ((bf16[2,2,128,1024]{3,2,1,0:T(8,128)(2,1)}), bf16[2,2,128,1024]{3,2,1,0:T(8,128)(2,1)}, u32[]{:S(2)}, u32[]{:S(2)}) async-start(bf16[2,2,128,1024]{3,2,1,0:T(8,128)(2,1)} %broadcast_in_dim.60), calls=%async_computation | async-start | bytes 2097152 | tf_op jit(solution)/shard_map/all_to_all | solution.py:30
  394.8 309.2 %all-reduce.7.cloned.1.call-start = ((), (), s32[]{:S(2)}) async-start(), calls=%async_computation.1 | async-start | bytes 7569408 | tf_op jit(solution)/shard_map/psum | solution.py:106
  397.1 3.3 copy-start.2
  400.4 20.9 %copy-start.6 = (bf16[256,512]{1,0:T(8,128)(2,1)}, bf16[256,512]{1,0:T(8,128)(2,1)S(1)}, u32[]{:S(2)}) copy-start(bf16[256,512]{1,0:T(8,128)(2,1)S(1)} %get-tuple-element.136) | copy-start | bytes 786436
  421.3 2.8 copy-start.7
  425.9 2.7 copy-start.4
  432.5 0.7 copy-start.12
  432.5 1.1 copy-start.3
  432.6 271.4 %copy-start.11 = (s32[4]{0:T(128)S(1)}, s32[4]{0:T(128)}, u32[]{:S(2)}) copy-start(s32[4]{0:T(128)} %get-tuple-element.267) | copy-start | bytes 52
  704.0 5.1 copy-start.5
Sparse Core Ops, SparseCore 0:
  13.9 48.5 all-reduce.8
  64.8 47.4 all-reduce.10
  115.0 50.1 all-reduce.12
  167.7 30.5 all-reduce.14
  205.0 45.3 all-reduce.8
  252.6 47.4 all-reduce.10
  302.8 50.1 all-reduce.12
  355.6 30.5 all-reduce.14
Sparse Core Ops, SparseCore 1:
  432.7 271.2 all-reduce.6
where the time goes:
time: 719 us; the launch traced here: 718 us
  waiting for transfers between devices  648 us (90%)
  local copies, waits for them, and re-layouts  18.8 us (3%)
  other arithmetic  16.4 us (2%)
  between operations  15.7 us (2%)
  matrix products  9.18 us (1%)
    psum x8, waiting for transfers between devices, broadcast_by_axis(): value = lax.psum(value, axis)  365 us
    psum x1, waiting for transfers between devices, body(): summed, rel_grad = lax.psum((candidate_gradient, rel_part), ENT_GRP)  267 us
    all_to_all x1, waiting for transfers between devices, copy_for_each(): return lax.all_to_all(copies, axis, split_axis=0, concat_axis=0, tiled=True)  15.2 us
  transfers between devices with their start and end apart: 10, of which 10 were waited for; matrix products, arithmetic and copies ran while one was open for 1% of the time, Pallas kernels for 0%

commit v1 on v0

v1 whole, which is shorter than its diff:
```python
import jax
import jax.numpy as jnp
from jax import lax
from jax.experimental import pallas as pl
from jax.experimental.pallas import tpu as pltpu
from jax.sharding import Mesh
from jax.sharding import PartitionSpec as P

BLK = 128
ENT = ("x", "y", "zl", "c")
ENT_GRP = ("x", "y", "zl", "c", "zh")
MESH = pl.DeviceIdType.MESH
BF = jnp.bfloat16
F32 = jnp.float32
SOFTMAX_TEMPER = 2.0
RELP = 832
RY = 208


class Spot:
    def __init__(self):
        self.x = lax.axis_index("x")
        self.y = lax.axis_index("y")
        self.c = lax.axis_index("c")
        self.zl = lax.axis_index("zl")
        self.zh = lax.axis_index("zh")
        self.z = self.zh * 4 + self.zl

    def xs(self, k):
        t = lax.rem(self.x + k, 4)
        return t, {"x": t}

    def ys(self, k):
        t = lax.rem(self.y + k, 4)
        return t, {"y": t}

    def zs(self, k):
        t = lax.rem(self.z + k, 8)
        return t, {"zh": lax.div(t, 4), "zl": lax.rem(t, 4)}

    def partner(self):
        return {"c": 1 - self.c}

    def greet(self):
        barrier = pltpu.get_barrier_semaphore()
        peers = [self.partner()]
        peers += [self.xs(k)[1] for k in range(1, 4)]
        peers += [self.ys(k)[1] for k in range(1, 4)]
        peers += [self.zs(k)[1] for k in range(1, 8)]
        for peer in peers:
            pl.semaphore_signal(barrier, inc=1, device_id=peer, device_id_type=MESH)
        pl.semaphore_wait(barrier, len(peers))


class Links:
    def __init__(self, send, recv):
        self.send, self.recv, self.used, self.sent = send, recv, 0, []

    def go(self, src, dst, device):
        n = self.used
        self.used += 1
        copy = pltpu.make_async_remote_copy(
            src_ref=src, dst_ref=dst, send_sem=self.send.at[n], recv_sem=self.recv.at[n],
            device_id=device, device_id_type=MESH,
        )
        copy.start()
        self.sent.append(copy)
        return copy

    def drain(self):
        for copy in self.sent:
            copy.wait_send()


def tile(start, size, unit):
    return pl.ds(pl.multiple_of(start, unit), size)


N_BCAST = 64


def bcast_kernel(owner_s, local_s, table_hbm, cand_hbm, table_v, stage, pbuf, sel, r0, r1, t0, t1,
                 q0, q1, zb, cand, send, recv, sem):
    me = Spot()
    x, y, z, c = me.x, me.y, me.z, me.c
    fetch = pltpu.make_async_copy(table_hbm, table_v, sem.at[0])
    fetch.start()
    me.greet()
    fetch.wait()
    links = Links(send, recv)
    entity = ((x * 4 + y) * 4 + me.zl) * 2 + c
    for j in range(2):
        b = me.zh * 2 + j
        held = (owner_s[b] == entity).astype(jnp.int32)
        masks = [
            (held * (local_s[b] == n).astype(jnp.int32)).astype(F32).astype(BF) for n in range(4)
        ]
        for r in range(0, BLK, 16):
            total = table_v[pl.ds(r, 16), :] * masks[0]
            for n in range(1, 4):
                total = total + table_v[pl.ds(n * BLK + r, 16), :] * masks[n]
            stage[j, pl.ds(r, 16), :] = total
    swaps = [
        links.go(stage.at[j, tile((1 - c) * 64, 64, 64), :], pbuf.at[j], me.partner())
        for j in range(2)
    ]
    for j in range(2):
        swaps[j].wait_recv()
        sel[j] = stage[j, tile(c * 64, 64, 64), :] + pbuf[j]
    first = [[], []]
    for k in range(1, 4):
        to, dev = me.xs(k)
        first[0].append(links.go(sel.at[0, :, tile(to * 256, 256, 256)], r0.at[k], dev))
        to, dev = me.ys(k)
        first[1].append(links.go(sel.at[1, tile(to * 16, 16, 16), :], r1.at[k], dev))
    r0[0] = sel[0, :, tile(x * 256, 256, 256)]
    r1[0] = sel[1, tile(y * 16, 16, 16), :]
    for copy in first[0]:
        copy.wait_recv()
    t0[...] = (r0[0] + r0[1]) + (r0[2] + r0[3])
    second = [[], []]
    for k in range(1, 4):
        to, dev = me.ys(k)
        second[0].append(links.go(t0.at[tile(to * 16, 16, 16), :], q0.at[k], dev))
    q0[0] = t0[tile(y * 16, 16, 16), :]
    for copy in first[1]:
        copy.wait_recv()
    t1[...] = (r1[0] + r1[1]) + (r1[2] + r1[3])
    for k in range(1, 4):
        to, dev = me.xs(k)
        second[1].append(links.go(t1.at[:, tile(to * 256, 256, 256)], q1.at[k], dev))
    q1[0] = t1[:, tile(x * 256, 256, 256)]
    for copy in second[0]:
        copy.wait_recv()
    zb[0, 0] = (q0[0] + q0[1]) + (q0[2] + q0[3])
    for copy in second[1]:
        copy.wait_recv()
    zb[0, 1] = (q1[0] + q1[1]) + (q1[2] + q1[3])
    third = []
    for k in range(1, 8):
        to, dev = me.zs(k)
        third.append(links.go(zb.at[0], zb.at[k], dev))
    for copy in third:
        copy.wait_recv()
    here = (tile(c * 64 + y * 16, 16, 16), tile(x * 256, 256, 256))
    zeros = jnp.zeros((16, 256), BF)
    for j in range(2):
        half = [zeros, zeros]
        for k in range(8):
            isl = (lax.rem(z - k + 8, 8) < 4).astype(jnp.int32)
            low = isl.astype(F32).astype(BF)
            high = (1 - isl).astype(F32).astype(BF)
            piece = zb[k, j]
            half[0] = half[0] + piece * low
            half[1] = half[1] + piece * high
        for h in range(2):
            cand[h, j, here[0], here[1]] = half[h]
    fourth = [[], []]
    for k in range(1, 4):
        spot = cand.at[:, 0, here[0], here[1]]
        fourth[0].append(links.go(spot, spot, me.ys(k)[1]))
        spot = cand.at[:, 1, here[0], here[1]]
        fourth[1].append(links.go(spot, spot, me.xs(k)[1]))
    fifth = [[], []]
    forward = [[], []]

    def slab0(xx):
        return cand.at[:, 0, tile(c * 64, 64, 64), tile(xx * 256, 256, 256)]

    def slab1(yy):
        return cand.at[:, 1, tile(c * 64 + yy * 16, 16, 16), :]

    for copy in fourth[0]:
        copy.wait_recv()
    for k in range(1, 4):
        fifth[0].append(links.go(slab0(x), slab0(x), me.xs(k)[1]))
    for copy in fourth[1]:
        copy.wait_recv()
    for k in range(1, 4):
        fifth[1].append(links.go(slab1(y), slab1(y), me.ys(k)[1]))
    forward[0].append(links.go(slab0(x), slab0(x), me.partner()))
    forward[1].append(links.go(slab1(y), slab1(y), me.partner()))
    for k in (1, 3, 2):
        fifth[0][k - 1].wait_recv()
        xx = lax.rem(x - k + 4, 4)
        forward[0].append(links.go(slab0(xx), slab0(xx), me.partner()))
        fifth[1][k - 1].wait_recv()
        yy = lax.rem(y - k + 4, 4)
        forward[1].append(links.go(slab1(yy), slab1(yy), me.partner()))
    for j in range(2):
        for copy in forward[j]:
            copy.wait_recv()
    out = pltpu.make_async_copy(cand, cand_hbm, sem.at[1])
    out.start()
    links.drain()
    out.wait()


def broadcast(owner, local, table):
    smem = pl.BlockSpec(memory_space=pltpu.SMEM)
    anyw = pl.BlockSpec(memory_space=pl.ANY)
    return pl.pallas_call(
        bcast_kernel,
        out_shape=jax.ShapeDtypeStruct((2, 2, 128, 1024), BF),
        in_specs=[smem, smem, anyw],
        out_specs=anyw,
        scratch_shapes=[
            pltpu.VMEM((512, 1024), BF),
            pltpu.VMEM((2, 128, 1024), BF),
            pltpu.VMEM((2, 64, 1024), BF),
            pltpu.VMEM((2, 64, 1024), BF),
            pltpu.VMEM((4, 64, 256), BF),
            pltpu.VMEM((4, 16, 1024), BF),
            pltpu.VMEM((64, 256), BF),
            pltpu.VMEM((16, 1024), BF),
            pltpu.VMEM((4, 16, 256), BF),
            pltpu.VMEM((4, 16, 256), BF),
            pltpu.VMEM((8, 2, 16, 256), BF),
            pltpu.VMEM((2, 2, 128, 1024), BF),
            pltpu.SemaphoreType.DMA((N_BCAST,)),
            pltpu.SemaphoreType.DMA((N_BCAST,)),
            pltpu.SemaphoreType.DMA((2,)),
        ],
        compiler_params=pltpu.CompilerParams(collective_id=0, has_side_effects=True),
    )(owner, local, table)


N_RED = 72


def reduce_kernel(a_ref, b_ref, ga_hbm, gb_hbm, pa, pb, a1, b1, ra, rb, a2, b2, ra2, rb2, a3, b3,
                  raz, rbz, ga, gb, send, recv, sem):
    me = Spot()
    x, y, z, c = me.x, me.y, me.z, me.c
    me.greet()
    links = Links(send, recv)
    swap_a = links.go(a_ref.at[tile((1 - c) * 256, 256, 256), :], pa, me.partner())
    swap_b = links.go(b_ref.at[:, tile((1 - c) * 256, 256, 256)], pb, me.partner())
    swap_a.wait_recv()
    a1[...] = (a_ref[tile(c * 256, 256, 256), :].astype(F32) + pa[...].astype(F32)).astype(BF)
    one_a, one_b = [], []
    for k in (2, 1, 3):
        to, dev = me.xs(k)
        one_a.append(links.go(a1.at[:, tile(to * 256, 256, 256)], ra.at[k - 1], dev))
    swap_b.wait_recv()
    b1[...] = (b_ref[:, tile(c * 256, 256, 256)].astype(F32) + pb[...].astype(F32)).astype(BF)
    for k in (2, 1, 3):
        to, dev = me.ys(k)
        one_b.append(links.go(b1.at[tile(to * RY, RY, 16), :], rb.at[k - 1], dev))
    for copy in one_a:
        copy.wait_recv()
    total = a1[:, tile(x * 256, 256, 256)].astype(F32)
    for k in range(3):
        total = total + ra[k].astype(F32)
    a2[...] = total.astype(BF)
    two_a, two_b = [], []
    for k in (2, 1, 3):
        to, dev = me.ys(k)
        two_a.append(links.go(a2.at[tile(to * 64, 64, 64), :], ra2.at[k - 1], dev))
    for copy in one_b:
        copy.wait_recv()
    total = b1[tile(y * RY, RY, 16), :].astype(F32)
    for k in range(3):
        total = total + rb[k].astype(F32)
    b2[pl.ds(0, RY), :] = total.astype(BF)
    b2[pl.ds(RY, 256 - RY), :] = jnp.zeros((256 - RY, 256), BF)
    for k in (2, 1, 3):
        to, dev = me.xs(k)
        two_b.append(links.go(b2.at[tile(to * 64, 64, 64), :], rb2.at[k - 1], dev))

    def zcell(t):
        return tile(lax.div(t, 2) * 16, 16, 16), tile(lax.rem(t, 2) * 128, 128, 128)

    three_a, three_b = [], []
    for copy in two_a:
        copy.wait_recv()
    total = a2[tile(y * 64, 64, 64), :].astype(F32)
    for k in range(3):
        total = total + ra2[k].astype(F32)
    a3[...] = total.astype(BF)
    for k in (4, 3, 5, 2, 6, 1, 7):
        to, dev = me.zs(k)
        three_a.append(links.go(a3.at[zcell(to)], raz.at[k - 1], dev))
    for copy in two_b:
        copy.wait_recv()
    total = b2[tile(x * 64, 64, 64), :].astype(F32)
    for k in range(3):
        total = total + rb2[k].astype(F32)
    b3[...] = total.astype(BF)
    for k in (4, 3, 5, 2, 6, 1, 7):
        to, dev = me.zs(k)
        three_b.append(links.go(b3.at[zcell(to)], rbz.at[k - 1], dev))

    zr, zc = lax.div(z, 2) * 16, lax.rem(z, 2) * 128

    def a_cell():
        return ga.at[tile(c * 256 + y * 64 + zr, 16, 16), tile(x * 256 + zc, 128, 128)]

    def b_cell():
        return gb.at[y, tile(x * 64 + zr, 16, 16), tile(c * 256 + zc, 128, 128)]

    four_a, four_b = [], []
    for copy in three_a:
        copy.wait_recv()
    total = a3[zcell(z)].astype(F32)
    for k in range(7):
        total = total + raz[k].astype(F32)
    a_cell()[...] = total.astype(BF)
    for k in (4, 3, 5, 2, 6, 1, 7):
        four_a.append(links.go(a_cell(), a_cell(), me.zs(k)[1]))
    for copy in three_b:
        copy.wait_recv()
    total = b3[zcell(z)].astype(F32)
    for k in range(7):
        total = total + rbz[k].astype(F32)
    b_cell()[...] = total.astype(BF)
    for k in (4, 3, 5, 2, 6, 1, 7):
        four_b.append(links.go(b_cell(), b_cell(), me.zs(k)[1]))

    five_a, five_b = [], []
    for copy in four_a:
        copy.wait_recv()
    spot = ga.at[tile(c * 256 + y * 64, 64, 64), tile(x * 256, 256, 256)]
    for k in (2, 1, 3):
        five_a.append(links.go(spot, spot, me.ys(k)[1]))
    for copy in four_b:
        copy.wait_recv()
    spot = gb.at[y, tile(x * 64, 64, 64), tile(c * 256, 256, 256)]
    for k in (2, 1, 3):
        five_b.append(links.go(spot, spot, me.xs(k)[1]))

    def slab_a(xx):
        return ga.at[tile(c * 256, 256, 256), tile(xx * 256, 256, 256)]

    def slab_b(yy):
        return gb.at[yy, pl.ds(0, RY), tile(c * 256, 256, 256)]

    six_a, six_b, last = {}, {}, []
    for copy in five_a:
        copy.wait_recv()
    for k in (2, 1, 3):
        six_a[k] = links.go(slab_a(x), slab_a(x), me.xs(k)[1])
    last.append(links.go(slab_a(x), slab_a(x), me.partner()))
    for copy in five_b:
        copy.wait_recv()
    for k in (2, 1, 3):
        six_b[k] = links.go(slab_b(y), slab_b(y), me.ys(k)[1])
    last.append(links.go(slab_b(y), slab_b(y), me.partner()))
    for k in (1, 3, 2):
        six_a[k].wait_recv()
        xx = lax.rem(x - k + 4, 4)
        last.append(links.go(slab_a(xx), slab_a(xx), me.partner()))
        six_b[k].wait_recv()
        yy = lax.rem(y - k + 4, 4)
        last.append(links.go(slab_b(yy), slab_b(yy), me.partner()))
    for copy in last:
        copy.wait_recv()
    outs = [
        pltpu.make_async_copy(ga, ga_hbm, sem.at[0]),
        pltpu.make_async_copy(gb.at[:, pl.ds(0, RY), :], gb_hbm, sem.at[1]),
    ]
    for copy in outs:
        copy.start()
    links.drain()
    for copy in outs:
        copy.wait()


def all_reduce(a, b):
    anyw = pl.BlockSpec(memory_space=pl.ANY)
    vmem = pl.BlockSpec(memory_space=pltpu.VMEM)
    return pl.pallas_call(
        reduce_kernel,
        out_shape=(
            jax.ShapeDtypeStruct((512, 1024), BF),
            jax.ShapeDtypeStruct((4, RY, 512), BF),
        ),
        in_specs=[vmem, vmem],
        out_specs=(anyw, anyw),
        scratch_shapes=[
            pltpu.VMEM((256, 1024), BF),
            pltpu.VMEM((RELP, 256), BF),
            pltpu.VMEM((256, 1024), BF),
            pltpu.VMEM((RELP, 256), BF),
            pltpu.VMEM((3, 256, 256), BF),
            pltpu.VMEM((3, RY, 256), BF),
            pltpu.VMEM((256, 256), BF),
            pltpu.VMEM((256, 256), BF),
            pltpu.VMEM((3, 64, 256), BF),
            pltpu.VMEM((3, 64, 256), BF),
            pltpu.VMEM((64, 256), BF),
            pltpu.VMEM((64, 256), BF),
            pltpu.VMEM((7, 16, 128), BF),
            pltpu.VMEM((7, 16, 128), BF),
            pltpu.VMEM((512, 1024), BF),
            pltpu.VMEM((4, 256, 512), BF),
            pltpu.SemaphoreType.DMA((N_RED,)),
            pltpu.SemaphoreType.DMA((N_RED,)),
            pltpu.SemaphoreType.DMA((2,)),
        ],
        compiler_params=pltpu.CompilerParams(collective_id=1, has_side_effects=True),
    )(a, b)


def body(entity_table, rel_phases, head_ids, rel_ids, target_pos, block_owner, block_local):
    half_dim = rel_phases.shape[1]
    rel_count = rel_phases.shape[0]
    shard_rows = entity_table.shape[0]
    blocks_total = block_owner.shape[0]
    fetched = broadcast(block_owner, block_local, entity_table)
    candidate_block = fetched.reshape(blocks_total * BLK, 2 * half_dim)
    heads = jnp.take(entity_table, head_ids, axis=0).astype(jnp.float32)
    angles = jnp.take(rel_phases, rel_ids, axis=0)
    cosine = jnp.cos(angles)
    sine = jnp.sin(angles)
    real_head = heads[:, :half_dim]
    imag_head = heads[:, half_dim:]
    real_query = real_head * cosine - imag_head * sine
    imag_query = real_head * sine + imag_head * cosine
    query_reduced_precision = jnp.concatenate([real_query, imag_query], axis=1).astype(jnp.bfloat16)
    candidate_norm = jnp.sum(jnp.square(candidate_block.astype(jnp.float32)), axis=1)
    inner_products = lax.dot_general(
        query_reduced_precision,
        candidate_block,
        (((1,), (1,)), ((), ())),
        preferred_element_type=jnp.float32,
    )
    logit_scores = (2.0 * inner_products - candidate_norm[None, :]) / SOFTMAX_TEMPER
    top = jnp.max(logit_scores, axis=1, keepdims=True)
    log_total = top[:, 0] + jnp.log(jnp.sum(jnp.exp(logit_scores - top), axis=1))
    picked = jnp.take_along_axis(logit_scores, target_pos[:, None], axis=1)[:, 0]
    losses = log_total - picked
    columns = jnp.arange(logit_scores.shape[1], dtype=jnp.int32)
    onehot = (columns[None, :] == target_pos[:, None]).astype(jnp.float32)
    softmax_weights = jnp.exp(logit_scores - log_total[:, None]) - onehot
    weights_reduced_precision = softmax_weights.astype(jnp.bfloat16)
    query_gradient = (
        2.0
        / SOFTMAX_TEMPER
        * jnp.dot(weights_reduced_precision, candidate_block, preferred_element_type=jnp.float32)
    )
    back_products = lax.dot_general(
        weights_reduced_precision,
        query_reduced_precision,
        (((0,), (0,)), ((), ())),
        preferred_element_type=jnp.float32,
    )
    candidate_gradient = (
        2.0
        / SOFTMAX_TEMPER
        * (
            back_products
            - jnp.sum(softmax_weights, axis=0)[:, None] * candidate_block.astype(jnp.float32)
        )
    )
    real_grad = query_gradient[:, :half_dim]
    imag_grad = query_gradient[:, half_dim:]
    head_grad = jnp.concatenate(
        [real_grad * cosine + imag_grad * sine, imag_grad * cosine - real_grad * sine], axis=1
    ).astype(jnp.bfloat16)
    angle_grad = imag_grad * real_query - real_grad * imag_query
    rel_part = jax.ops.segment_sum(angle_grad, rel_ids, num_segments=RELP)
    summed, rel_sum = all_reduce(candidate_gradient.astype(BF), rel_part.astype(BF))
    rel_grad = rel_sum.reshape(RELP, half_dim)[:rel_count].astype(F32)
    block_numbers = jnp.arange(shard_rows // BLK, dtype=jnp.int32)
    selector = (
        (block_owner == lax.axis_index(ENT))[:, None]
        & (block_local[:, None] == block_numbers[None, :])
    )
    blocks = summed.reshape(blocks_total, 1, BLK, 2 * half_dim).astype(F32)
    placed = jnp.sum(jnp.where(selector[:, :, None, None], blocks, 0.0), axis=0)
    table_grad = placed.reshape(shard_rows, 2 * half_dim).astype(jnp.bfloat16)
    return (losses, head_grad, table_grad, rel_grad)


def solution(mesh):
    finer = Mesh(mesh.devices.reshape(4, 4, 4, 2, mesh.shape["grp"]), ENT_GRP)
    placed = (P(ENT, None), P(), P(ENT_GRP), P(ENT_GRP), P(ENT_GRP), P(), P())
    return jax.shard_map(
        body,
        mesh=finer,
        in_specs=placed,
        out_specs=(P(ENT_GRP), P(ENT_GRP, None), P(ENT, None), P()),
        check_vma=False,
    )
```

time: 719 us -> 117 us (0.16)
  waiting for transfers between devices: 648 us -> 0 us
  Pallas kernels: 0 us -> 79.3 us
  between operations: 15.7 us -> 0.82 us
  local copies, waits for them, and re-layouts: 18.8 us -> 6.55 us
  other arithmetic: 16.4 us -> 24.9 us
    psum x9 -> x0, waiting for transfers between devices: 633 us -> none  [the longest x8 365 us: broadcast_by_axis(): value = lax.psum(value, axis)]
    pallas_call x0 -> x2, Pallas kernels: none -> 79.3 us  [the longest x1 42 us: all_reduce(): pl.pallas_call(reduce_kernel, out_shape=(jax.ShapeDtypeStruct((512, 1024)...]
    all_to_all x1 -> x0, waiting for transfers between devices: 15.2 us -> none  [copy_for_each(): return lax.all_to_all(copies, axis, split_axis=0, concat_axis=0, tiled=True)]
  transfers between devices with their start and end apart: 10 -> 0, of which waited for: 10 -> 0; matrix products, arithmetic and copies ran while one was open for 1% -> 0% of each run, Pallas kernels for 0% -> 0%
where the time goes in v1:
time: 117 us
  Pallas kernels  79.3 us (68%)
  other arithmetic  24.9 us (21%)
  local copies, waits for them, and re-layouts  6.55 us (6%)
  matrix products  5.01 us (4%)
    pallas_call x1, Pallas kernels, all_reduce(): pl.pallas_call(reduce_kernel, out_shape=(jax.ShapeDtypeStruct((512, 1024)...  42 us
    pallas_call x1, Pallas kernels, broadcast(): pl.pallas_call(bcast_kernel, out_shape=jax.ShapeDtypeStruct((2, 2, 128, 1...  37.3 us
    another operation x2, other arithmetic  6.2 us
    scatter-add x1, other arithmetic, body(): rel_part = jax.ops.segment_sum(angle_grad, rel_ids, num_segments=RELP)  3.57 us
    convert_element_type x1, other arithmetic, body(): rel_grad = rel_sum.reshape(RELP, half_dim)[:rel_count].astype(F32)  2.65 us
    dot_general x1, matrix products, body(): lax.dot_general(weights_reduced_precision, query_reduced_precision, (((0,...  2.53 us
    gather x1, local copies, waits for them, and re-layouts, body(): jnp.take_along_axis(logit_scores, target_pos[:, None], axis=1)[:, 0]  2.35 us

profile of v1, /device:TPU:1, one launch (start us, length us, event | category | flops | bytes accessed | tf_op | source)
XLA Modules:
  0.0 116.6 jit_solution(4155048313338390881)
XLA Ops:
  0.6 0.0 copy-start
  0.7 0.8 broadcast_compare_fusion
  1.4 0.7 fusion.11
  2.2 0.7 compare_and_fusion
  2.9 0.7 compare_and_fusion.1
  3.5 0.7 compare_select_fusion.2
  4.2 0.7 compare_select_fusion.1
  4.9 0.7 compare_select_fusion
  5.6 0.0 copy-done
  5.6 0.0 copy-start.1
  5.7 1.0 gather_fusion.1
  6.6 0.2 copy-done.1
  6.9 0.0 copy-start.4
  6.9 2.0 %gather_fusion = bf16[256,1024]{1,0:T(8,128)(2,1)} fusion(bf16[512,1024]{1,0:T(8,128)(2,1)S(1)} %copy-done.1, s32[1024]{0:T(1024)S(1)} %pad_clamp_fusion.1), kind=kCustom, calls=%fused_computation | custom fusion | bytes 1049600 | tf_op jit(solution)/shard_map/jit(_take)/gather | solution.py:412
  8.8 1.2 %select_convert_fusion = f32[256,1024]{1,0:T(8,128)S(1)} fusion(bf16[256,1024]{1,0:T(8,128)(2,1)} %gather_fusion, pred[256]{0:T(512)(128)(4,1)S(1)} %compare_and_fusion.1), kind=kLoop, calls=%fused_computation.25 | loop fusion | flops 524288 | bytes 1573120 | tf_op jit(solution)/shard_map/convert_element_type | solution.py:412
  10.0 0.0 copy-done.4
  10.0 3.2 %fusion.21 = (bf16[256,512]{1,0:T(8,128)(2,1)S(1)}, f32[256,512]{1,0:T(8,128)}, bf16[256,512]{1,0:T(8,128)(2,1)}, f32[256,512]{1,0:T(8,128)}) fusion(f32[256,1024]{1,0:T(8,128)S(1)} %select_convert_fusion, f32[256,512]{1,0:T(8,128)S(1)} %gather_fusion.1, pred[256]{0:T(512)(128)(4,1)S(1)} %compare_and_fusion), kind=kLoop, calls=%fused_computation.55 | loop fusion | flops 1179648 | bytes 3145984 | tf_op jit(solution)/shard_map/convert.3
  13.2 37.3 %shard_map.102 = bf16[2,2,128,1024]{3,2,1,0:T(8,128)(2,1)} custom-call(s32[4]{0:T(128)} %owner_s.1, s32[4]{0:T(128)} %local_s.1, bf16[512,1024]{1,0:T(8,128)(2,1)} %table_hbm.1), custom_call_target="tpu_custom_call" | custom-call | tf_op jit(solution)/shard_map/pallas_call | solution.py:202
  50.5 1.5 %multiply_reduce_fusion = f32[2,2,128]{2,1,0:T(2,128)S(1)} fusion(bf16[2,2,128,1024]{3,2,1,0:T(8,128)(2,1)} %shard_map.102), kind=kLoop, calls=%fused_computation.6 | loop fusion | flops 1572352 | bytes 1050624 | tf_op jit(solution)/shard_map/reduce_sum | solution.py:421
  52.0 0.0 copy-start.9
  52.0 0.0 copy-start.2
  52.0 2.0 %fusion.23 = (f32[256]{0:T(256)S(1)}, f32[256,512]{1,0:T(8,128)S(1)}) fusion(f32[512]{0:T(512)S(1)} %bitcast.20, bf16[512,1024]{1,0:T(8,128)(2,1)} %bitcast.14, bf16[256,512]{1,0:T(8,128)(2,1)} %get-tuple-element.16, bf16[256,512]{1,0:T(8,128)(2,1)S(1)} %get-tuple-element.10), kind=kOutput, calls=%fused_computation.57 | convolution fusion | flops 270008064 | bytes 2100224 | tf_op jit(solution)/shard_map/dot_general | solution.py:422
  54.0 2.3 %gather_fusion.2 = f32[256]{0:T(256)S(1)} fusion(f32[256,512]{1,0:T(8,128)S(1)} %get-tuple-element.19, s32[256]{0:T(256)S(1)} %bitcast.13), kind=kCustom, calls=%fused_computation.2 | custom fusion | bytes 4096 | tf_op jit(solution)/shard_map/jit(take_along_axis)/gather | solution.py:431
  56.3 0.2 exponential_reduce_fusion
  56.6 0.0 copy-done.9
  56.6 0.6 fusion.12
  57.1 0.2 fusion.9
  57.3 0.0 copy-done.2
  57.4 2.5 %subtract_convert_fusion.a_ref = bf16[512,1024]{1,0:T(8,128)(2,1)} fusion(bf16[512,1024]{1,0:T(8,128)(2,1)S(1)} %bitcast.15, f32[512]{0:T(512)S(1)} %fusion.9, bf16[256,512]{1,0:T(8,128)(2,1)} %get-tuple-element.16, bf16[256,512]{1,0:T(8,128)(2,1)S(1)} %get-tuple-element.10, f32[256,512]{1,0:T(8,128)S(1)} %get-tuple-element.19, s32[256]{0:T(256)S(1)} %copy-done.9, ...), kind=kOutput, calls=%fused_computation.5 | convolution fusion | flops 272236544 | bytes 3149824 | tf_op jit(solution)/shard_map/dot_general | solution.py:442
  59.9 0.0 copy-start.5
  59.9 0.5 fusion.19
  60.4 0.0 copy-start.3
  60.4 1.0 copy-done.3
  61.4 0.0 copy-done.5
  61.4 3.0 %add_convert_fusion = (bf16[256,512]{1,0:T(8,128)(2,1)}, bf16[256,512]{1,0:T(8,128)(2,1)}) fusion(f32[256,1024]{1,0:T(8,128)S(1)} %fusion.19, f32[256,512]{1,0:T(8,128)S(1)} %copy-done.5, pred[256]{0:T(512)(128)(4,1)S(1)} %compare_and_fusion), kind=kLoop, calls=%fused_computation.19 | loop fusion | flops 1179648 | bytes 2097408 | tf_op jit(solution)/shard_map/convert.1
  64.4 3.6 %scatter_custom_fusion = f32[832,512]{1,0:T(8,128)S(1)} fusion(s32[256]{0:T(256)} %param.10, f32[]{:T(128)} %constant.64.clone.1, f32[256,512]{1,0:T(8,128)} %get-tuple-element.17, f32[256,512]{1,0:T(8,128)} %get-tuple-element.11, f32[256,1024]{1,0:T(8,128)} %copy-done.3), kind=kCustom, calls=%fused_computation.10 | custom fusion | flops 524288 | bytes 3801600 | tf_op jit(solution)/shard_map/scatter-add | solution.py:462
  68.0 0.0 copy-start.7
  68.0 0.0 copy-start.8
  68.0 1.0 convert_element_type.50.b_ref
  69.0 0.0 copy-done.7
  69.0 0.0 copy-done.8
  69.1 0.9 pad_maximum_fusion.1
  69.9 42.0 %shard_map.103 = (bf16[512,1024]{1,0:T(8,128)(2,1)}, bf16[4,208,512]{2,1,0:T(8,128)(2,1)}) custom-call(bf16[512,1024]{1,0:T(8,128)(2,1)} %subtract_convert_fusion.a_ref, bf16[832,512]{1,0:T(8,128)(2,1)} %convert_element_type.50.b_ref), custom_call_target="tpu_custom_call" | custom-call | tf_op jit(solution)/shard_map/pallas_call | solution.py:372
  111.9 0.0 copy-start.6
  111.9 2.7 %slice_convert_fusion = f32[822,512]{1,0:T(8,128)} fusion(bf16[832,512]{1,0:T(8,128)(2,1)} %bitcast.18), kind=kLoop, calls=%fused_computation.12 | loop fusion | flops 420864 | bytes 2525184 | tf_op jit(solution)/shard_map/convert_element_type | solution.py:464
  114.6 0.0 copy-done.6
  114.6 0.2 bitcast_convert_fusion
  114.8 1.8 %select_reduce_fusion = bf16[4,128,1024]{2,1,0:T(8,128)(2,1)} fusion(f32[4,128,1024]{2,1,0:T(8,128)S(1)} %bitcast_convert_fusion, pred[4,4]{1,0:T(4,128)(4,1)S(1)} %fusion.11), kind=kLoop, calls=%fused_computation.4 | loop fusion | flops 3670016 | bytes 3145744 | tf_op jit(solution)/shard_map/reduce_sum | solution.py:471
  (5 shorter events, 0.0 us)
Async XLA Ops:
  0.6 5.0 %copy-start = (f32[822,512]{1,0:T(8,128)S(1)}, f32[822,512]{1,0:T(8,128)}, u32[]{:S(2)}) copy-start(f32[822,512]{1,0:T(8,128)} %param.8) | copy-start | bytes 5050372
  5.6 1.2 %copy-start.1 = (bf16[512,1024]{1,0:T(8,128)(2,1)S(1)}, bf16[512,1024]{1,0:T(8,128)(2,1)}, u32[]{:S(2)}) copy-start(bf16[512,1024]{1,0:T(8,128)(2,1)} %table_hbm.1) | copy-start | bytes 3145732
  6.9 3.1 %copy-start.4 = (f32[256,512]{1,0:T(8,128)}, f32[256,512]{1,0:T(8,128)S(1)}, u32[]{:S(2)}) copy-start(f32[256,512]{1,0:T(8,128)S(1)} %gather_fusion.1) | copy-start | bytes 1572868
  52.0 4.6 %copy-start.9 = (s32[256]{0:T(256)S(1)}, s32[256]{0:T(256)}, u32[]{:S(2)}) copy-start(s32[256]{0:T(256)} %param.11) | copy-start | bytes 3076
  52.0 5.3 %copy-start.2 = (bf16[2,2,128,1024]{3,2,1,0:T(8,128)(2,1)S(1)}, bf16[2,2,128,1024]{3,2,1,0:T(8,128)(2,1)}, u32[]{:S(2)}) copy-start(bf16[2,2,128,1024]{3,2,1,0:T(8,128)(2,1)} %shard_map.102) | copy-start | bytes 3145732
  59.9 1.5 %copy-start.5 = (f32[256,512]{1,0:T(8,128)S(1)}, f32[256,512]{1,0:T(8,128)}, u32[]{:S(2)}) copy-start(f32[256,512]{1,0:T(8,128)} %copy-done.4) | copy-start | bytes 1572868
  60.4 1.0 copy-start.3
  68.0 1.0 copy-start.7
  68.0 1.0 copy-start.8
  111.9 2.7 %copy-start.6 = (bf16[512,1024]{1,0:T(8,128)(2,1)S(1)}, bf16[512,1024]{1,0:T(8,128)(2,1)}, u32[]{:S(2)}) copy-start(bf16[512,1024]{1,0:T(8,128)(2,1)} %get-tuple-element.6) | copy-start | bytes 3145732

commit v2 on v1

v2 whole, which is shorter than its diff:
```python
import jax
import jax.numpy as jnp
from jax import lax
from jax.experimental import pallas as pl
from jax.experimental.pallas import tpu as pltpu
from jax.sharding import Mesh
from jax.sharding import PartitionSpec as P

BLK = 128
ENT = ("x", "y", "zl", "c")
ENT_GRP = ("x", "y", "zl", "c", "zh")
MESH = pl.DeviceIdType.MESH
BF = jnp.bfloat16
F32 = jnp.float32
SOFTMAX_TEMPER = 2.0
RELP = 832
RY = 208


class Spot:
    def __init__(self):
        self.x = lax.axis_index("x")
        self.y = lax.axis_index("y")
        self.c = lax.axis_index("c")
        self.zl = lax.axis_index("zl")
        self.zh = lax.axis_index("zh")
        self.z = self.zh * 4 + self.zl

    def xs(self, k):
        t = lax.rem(self.x + k, 4)
        return t, {"x": t}

    def ys(self, k):
        t = lax.rem(self.y + k, 4)
        return t, {"y": t}

    def zs(self, k):
        t = lax.rem(self.z + k, 8)
        return t, {"zh": lax.div(t, 4), "zl": lax.rem(t, 4)}

    def partner(self):
        return {"c": 1 - self.c}

    def hello(self):
        barrier = pltpu.get_barrier_semaphore()
        peers = [self.partner()]
        peers += [self.xs(k)[1] for k in range(1, 4)]
        peers += [self.ys(k)[1] for k in range(1, 4)]
        peers += [self.zs(k)[1] for k in range(1, 8)]
        for peer in peers:
            pl.semaphore_signal(barrier, inc=1, device_id=peer, device_id_type=MESH)

    def everyone(self):
        pl.semaphore_wait(pltpu.get_barrier_semaphore(), 14)


class Links:
    def __init__(self, send, recv):
        self.send, self.recv, self.used, self.sent = send, recv, 0, []

    def go(self, src, dst, device):
        n = self.used
        self.used += 1
        copy = pltpu.make_async_remote_copy(
            src_ref=src, dst_ref=dst, send_sem=self.send.at[n], recv_sem=self.recv.at[n],
            device_id=device, device_id_type=MESH,
        )
        copy.start()
        self.sent.append(copy)
        return copy

    def drain(self):
        for copy in self.sent:
            copy.wait_send()


def tile(start, size, unit):
    return pl.ds(pl.multiple_of(start, unit), size)


RELK = 896
N_COPY = 112


def lanes_of(row):
    return jnp.transpose(jnp.broadcast_to(row.astype(F32), (128, 256)))


def dot(a, b):
    return jnp.dot(a, b, preferred_element_type=F32)


def step_kernel(owner_s, local_s, head_r, rel_r, target_r, table_hbm, phase_hbm,
                loss_o, head_o, ga, gb,
                table_v, phase_v, tail_v, ph0, ph1, ph2, ohh, ohr, q_v, qr_v, qi_v, cos_v, sin_v,
                stage, pbuf, sel, r0, r1, t0, t1, q0, q1, zb, cand,
                s_v, w_v, wt_v, sum_v, ang0, ang1, oht,
                asend, afull, pa, bsend, bfull, pb, a1, b1, ra, rb, a2f, b2f, a2, b2, ra2, rb2,
                a3f, b3f, a3, b3, raz, rbz, send, recv, sem):
    me = Spot()
    x, y, z, c = me.x, me.y, me.z, me.c
    fetch = pltpu.make_async_copy(table_hbm, table_v, sem.at[0])
    fetch.start()
    fetch_phase = pltpu.make_async_copy(phase_hbm, phase_v, sem.at[1])
    fetch_phase.start()
    me.hello()
    fetch.wait()
    links = Links(send, recv)
    entity = ((x * 4 + y) * 4 + me.zl) * 2 + c
    for j in range(2):
        b = me.zh * 2 + j
        held = (owner_s[b] == entity).astype(jnp.int32)
        masks = [
            (held * (local_s[b] == n).astype(jnp.int32)).astype(F32).astype(BF) for n in range(4)
        ]
        for r in range(0, BLK, 16):
            total = table_v[pl.ds(r, 16), :] * masks[0]
            for n in range(1, 4):
                total = total + table_v[pl.ds(n * BLK + r, 16), :] * masks[n]
            stage[j, pl.ds(r, 16), :] = total
    me.everyone()
    swaps = [
        links.go(stage.at[j, tile((1 - c) * 64, 64, 64), :], pbuf.at[j], me.partner())
        for j in range(2)
    ]

    def prepare():
        lane = lax.broadcasted_iota(jnp.int32, (256, 128), 1).astype(F32)
        ids = lanes_of(head_r[...])
        for g in range(4):
            ohh[:, pl.ds(g * 128, 128)] = (ids == lane + float(g * 128)).astype(F32).astype(BF)
        ids = lanes_of(rel_r[...])
        for g in range(7):
            ohr[:, pl.ds(g * 128, 128)] = (ids == lane + float(g * 128)).astype(F32).astype(BF)

    def split_phases():
        fetch_phase.wait()
        tail_v[...] = jnp.zeros((128, 512), F32)
        tail_v[pl.ds(0, 822 - 768), :] = phase_v[pl.ds(768, 822 - 768), :]
        for r in range(0, RELK, 128):
            rows = pl.ds(r, 128)
            value = phase_v[rows, :] if r < 768 else tail_v[...]
            top = value.astype(BF)
            value = value - top.astype(F32)
            ph0[rows, :] = top
            top = value.astype(BF)
            ph1[rows, :] = top
            ph2[rows, :] = (value - top.astype(F32)).astype(BF)

    def rotate(j):
        cols, more = pl.ds(j * 128, 128), pl.ds(512 + j * 128, 128)
        which = ohr[...]
        theta = dot(which, ph0[:, cols]) + (dot(which, ph1[:, cols]) + dot(which, ph2[:, cols]))
        cosine, sine = jnp.cos(theta), jnp.sin(theta)
        hr = dot(ohh[...], table_v[:, cols])
        hi = dot(ohh[...], table_v[:, more])
        qr = hr * cosine - hi * sine
        qi = hr * sine + hi * cosine
        cos_v[:, cols] = cosine
        sin_v[:, cols] = sine
        qr_v[:, cols] = qr
        qi_v[:, cols] = qi
        q_v[:, cols] = qr.astype(BF)
        q_v[:, more] = qi.astype(BF)

    prepare()
    for j in range(2):
        swaps[j].wait_recv()
        sel[j] = stage[j, tile(c * 64, 64, 64), :] + pbuf[j]
    first = [[], []]
    for k in range(1, 4):
        to, dev = me.xs(k)
        first[0].append(links.go(sel.at[0, :, tile(to * 256, 256, 256)], r0.at[k], dev))
        to, dev = me.ys(k)
        first[1].append(links.go(sel.at[1, tile(to * 16, 16, 16), :], r1.at[k], dev))
    r0[0] = sel[0, :, tile(x * 256, 256, 256)]
    r1[0] = sel[1, tile(y * 16, 16, 16), :]
    split_phases()
    rotate(0)
    for copy in first[0]:
        copy.wait_recv()
    t0[...] = (r0[0] + r0[1]) + (r0[2] + r0[3])
    second = [[], []]
    for k in range(1, 4):
        to, dev = me.ys(k)
        second[0].append(links.go(t0.at[tile(to * 16, 16, 16), :], q0.at[k], dev))
    q0[0] = t0[tile(y * 16, 16, 16), :]
    for copy in first[1]:
        copy.wait_recv()
    t1[...] = (r1[0] + r1[1]) + (r1[2] + r1[3])
    for k in range(1, 4):
        to, dev = me.xs(k)
        second[1].append(links.go(t1.at[:, tile(to * 256, 256, 256)], q1.at[k], dev))
    q1[0] = t1[:, tile(x * 256, 256, 256)]
    rotate(1)
    for copy in second[0]:
        copy.wait_recv()
    zb[0, 0] = (q0[0] + q0[1]) + (q0[2] + q0[3])
    for copy in second[1]:
        copy.wait_recv()
    zb[0, 1] = (q1[0] + q1[1]) + (q1[2] + q1[3])
    third = []
    for k in (4, 3, 5, 2, 6, 1, 7):
        to, dev = me.zs(k)
        third.append(links.go(zb.at[0], zb.at[k], dev))
    rotate(2)
    rotate(3)
    for copy in third:
        copy.wait_recv()
    here = (tile(c * 64 + y * 16, 16, 16), tile(x * 256, 256, 256))
    zeros = jnp.zeros((16, 256), BF)
    for j in range(2):
        half = [zeros, zeros]
        for k in range(8):
            isl = (lax.rem(z - k + 8, 8) < 4).astype(jnp.int32)
            low = isl.astype(F32).astype(BF)
            high = (1 - isl).astype(F32).astype(BF)
            piece = zb[k, j]
            half[0] = half[0] + piece * low
            half[1] = half[1] + piece * high
        for h in range(2):
            cand[h, j, here[0], here[1]] = half[h]
    fourth = [[], []]
    for k in (2, 1, 3):
        spot = cand.at[:, 0, here[0], here[1]]
        fourth[0].append(links.go(spot, spot, me.ys(k)[1]))
        spot = cand.at[:, 1, here[0], here[1]]
        fourth[1].append(links.go(spot, spot, me.xs(k)[1]))
    fifth = [{}, {}]
    forward = []

    def slab0(xx):
        return cand.at[:, 0, tile(c * 64, 64, 64), tile(xx * 256, 256, 256)]

    def slab1(yy):
        return cand.at[:, 1, tile(c * 64 + yy * 16, 16, 16), :]

    oht[...] = (
        lax.broadcasted_iota(jnp.int32, (RELP, 256), 0) == jnp.broadcast_to(rel_r[...], (RELP, 256))
    ).astype(F32).astype(BF)
    for copy in fourth[0]:
        copy.wait_recv()
    for k in (2, 1, 3):
        fifth[0][k] = links.go(slab0(x), slab0(x), me.xs(k)[1])
    for copy in fourth[1]:
        copy.wait_recv()
    for k in (2, 1, 3):
        fifth[1][k] = links.go(slab1(y), slab1(y), me.ys(k)[1])
    forward.append(links.go(slab0(x), slab0(x), me.partner()))
    forward.append(links.go(slab1(y), slab1(y), me.partner()))
    for k in (1, 3, 2):
        fifth[0][k].wait_recv()
        xx = lax.rem(x - k + 4, 4)
        forward.append(links.go(slab0(xx), slab0(xx), me.partner()))
        fifth[1][k].wait_recv()
        yy = lax.rem(y - k + 4, 4)
        forward.append(links.go(slab1(yy), slab1(yy), me.partner()))
    for copy in forward:
        copy.wait_recv()

    for h in range(2):
        for j in range(2):
            block = cand[h, j]
            wide = block.astype(F32)
            norm = jnp.sum(wide * wide, axis=1, keepdims=True)
            inner = lax.dot_general(
                block, q_v[...], (((1,), (1,)), ((), ())), preferred_element_type=F32
            )
            s_v[pl.ds((2 * h + j) * BLK, BLK), :] = inner - norm / SOFTMAX_TEMPER
    scores = s_v[...]
    top = jnp.max(scores, axis=0, keepdims=True)
    log_total = top + jnp.log(jnp.sum(jnp.exp(scores - top), axis=0, keepdims=True))
    mark = (
        lax.broadcasted_iota(jnp.int32, (512, 256), 0) == jnp.broadcast_to(target_r[...], (512, 256))
    )
    loss_o[...] = log_total - jnp.sum(jnp.where(mark, scores, 0.0), axis=0, keepdims=True)
    weights = jnp.exp(scores - log_total) - mark.astype(F32)
    w_v[...] = weights.astype(BF)
    sum_v[...] = jnp.broadcast_to(jnp.sum(weights, axis=1, keepdims=True), (512, 128))

    def back(block):
        rows = tile(block * BLK, BLK, BLK)
        h, j = lax.div(block, 2), lax.rem(block, 2)
        return dot(w_v[rows, :], q_v[...]) - sum_v[rows, 0:1] * cand[h, j].astype(F32)

    for j in range(2):
        asend[pl.ds(j * BLK, BLK), :] = back((1 - c) * 2 + j).astype(BF)
    swap_a = links.go(asend, pa, me.partner())
    for j in range(2):
        afull[pl.ds(j * BLK, BLK), :] = back(c * 2 + j)
    wt_v[...] = jnp.transpose(weights).astype(BF)
    swap_a.wait_recv()
    a1[...] = (afull[...] + pa[...].astype(F32)).astype(BF)
    one_a, one_b = [], []
    for k in (2, 1, 3):
        to, dev = me.xs(k)
        one_a.append(links.go(a1.at[:, tile(to * 256, 256, 256)], ra.at[k - 1], dev))

    for j in range(4):
        cols, more = pl.ds(j * 128, 128), pl.ds(512 + j * 128, 128)
        dqr = dot(wt_v[...], cand[:, :, :, cols].reshape(512, 128))
        dqi = dot(wt_v[...], cand[:, :, :, more].reshape(512, 128))
        cosine, sine = cos_v[:, cols], sin_v[:, cols]
        head_o[:, cols] = (dqr * cosine + dqi * sine).astype(BF)
        head_o[:, more] = (dqi * cosine - dqr * sine).astype(BF)
        angle = dqi * qr_v[:, cols] - dqr * qi_v[:, cols]
        top = angle.astype(BF)
        ang0[:, cols] = top
        ang1[:, cols] = (angle - top.astype(F32)).astype(BF)

    def rel_half(half):
        cols = tile(half * 256, 256, 256)
        return dot(oht[...], ang0[:, cols]) + dot(oht[...], ang1[:, cols])

    bsend[...] = rel_half(1 - c).astype(BF)
    swap_b = links.go(bsend, pb, me.partner())
    bfull[...] = rel_half(c)
    swap_b.wait_recv()
    b1[...] = (bfull[...] + pb[...].astype(F32)).astype(BF)
    for k in (2, 1, 3):
        to, dev = me.ys(k)
        one_b.append(links.go(b1.at[tile(to * RY, RY, 16), :], rb.at[k - 1], dev))
    for copy in one_a:
        copy.wait_recv()
    mine = tile(x * 256, 256, 256)
    total = afull[:, mine] + pa[:, mine].astype(F32)
    for k in range(3):
        total = total + ra[k].astype(F32)
    a2f[...] = total
    a2[...] = total.astype(BF)
    two_a, two_b = [], []
    for k in (2, 1, 3):
        to, dev = me.ys(k)
        two_a.append(links.go(a2.at[tile(to * 64, 64, 64), :], ra2.at[k - 1], dev))
    for copy in one_b:
        copy.wait_recv()
    mine = tile(y * RY, RY, 16)
    total = bfull[mine, :] + pb[mine, :].astype(F32)
    for k in range(3):
        total = total + rb[k].astype(F32)
    b2f[pl.ds(0, RY), :] = total
    b2[pl.ds(0, RY), :] = total.astype(BF)
    b2f[pl.ds(RY, 256 - RY), :] = jnp.zeros((256 - RY, 256), F32)
    b2[pl.ds(RY, 256 - RY), :] = jnp.zeros((256 - RY, 256), BF)
    for k in (2, 1, 3):
        to, dev = me.xs(k)
        two_b.append(links.go(b2.at[tile(to * 64, 64, 64), :], rb2.at[k - 1], dev))

    def zcell(t):
        return tile(lax.div(t, 2) * 16, 16, 16), tile(lax.rem(t, 2) * 128, 128, 128)

    three_a, three_b = [], []
    for copy in two_a:
        copy.wait_recv()
    total = a2f[tile(y * 64, 64, 64), :]
    for k in range(3):
        total = total + ra2[k].astype(F32)
    a3f[...] = total
    a3[...] = total.astype(BF)
    for k in (4, 3, 5, 2, 6, 1, 7):
        to, dev = me.zs(k)
        three_a.append(links.go(a3.at[zcell(to)], raz.at[k - 1], dev))
    for copy in two_b:
        copy.wait_recv()
    total = b2f[tile(x * 64, 64, 64), :]
    for k in range(3):
        total = total + rb2[k].astype(F32)
    b3f[...] = total
    b3[...] = total.astype(BF)
    for k in (4, 3, 5, 2, 6, 1, 7):
        to, dev = me.zs(k)
        three_b.append(links.go(b3.at[zcell(to)], rbz.at[k - 1], dev))

    zr, zc = lax.div(z, 2) * 16, lax.rem(z, 2) * 128

    def a_cell():
        return ga.at[tile(c * 256 + y * 64 + zr, 16, 16), tile(x * 256 + zc, 128, 128)]

    def b_cell():
        return gb.at[y, tile(x * 64 + zr, 16, 16), tile(c * 256 + zc, 128, 128)]

    four_a, four_b = [], []
    for copy in three_a:
        copy.wait_recv()
    total = a3f[zcell(z)]
    for k in range(7):
        total = total + raz[k].astype(F32)
    a_cell()[...] = total.astype(BF)
    for k in (4, 3, 5, 2, 6, 1, 7):
        four_a.append(links.go(a_cell(), a_cell(), me.zs(k)[1]))
    for copy in three_b:
        copy.wait_recv()
    total = b3f[zcell(z)]
    for k in range(7):
        total = total + rbz[k].astype(F32)
    b_cell()[...] = total.astype(BF)
    for k in (4, 3, 5, 2, 6, 1, 7):
        four_b.append(links.go(b_cell(), b_cell(), me.zs(k)[1]))

    five_a, five_b = [], []
    for copy in four_a:
        copy.wait_recv()
    spot = ga.at[tile(c * 256 + y * 64, 64, 64), tile(x * 256, 256, 256)]
    for k in (2, 1, 3):
        five_a.append(links.go(spot, spot, me.ys(k)[1]))
    for copy in four_b:
        copy.wait_recv()
    spot = gb.at[y, tile(x * 64, 64, 64), tile(c * 256, 256, 256)]
    for k in (2, 1, 3):
        five_b.append(links.go(spot, spot, me.xs(k)[1]))

    def slab_a(xx):
        return ga.at[tile(c * 256, 256, 256), tile(xx * 256, 256, 256)]

    def slab_b(yy):
        return gb.at[yy, pl.ds(0, RY), tile(c * 256, 256, 256)]

    six_a, six_b, last = {}, {}, []
    for copy in five_a:
        copy.wait_recv()
    for k in (2, 1, 3):
        six_a[k] = links.go(slab_a(x), slab_a(x), me.xs(k)[1])
    last.append(links.go(slab_a(x), slab_a(x), me.partner()))
    for copy in five_b:
        copy.wait_recv()
    for k in (2, 1, 3):
        six_b[k] = links.go(slab_b(y), slab_b(y), me.ys(k)[1])
    last.append(links.go(slab_b(y), slab_b(y), me.partner()))
    for k in (1, 3, 2):
        six_a[k].wait_recv()
        xx = lax.rem(x - k + 4, 4)
        last.append(links.go(slab_a(xx), slab_a(xx), me.partner()))
        six_b[k].wait_recv()
        yy = lax.rem(y - k + 4, 4)
        last.append(links.go(slab_b(yy), slab_b(yy), me.partner()))
    for copy in last:
        copy.wait_recv()
    links.drain()


def step(owner, local, head, rel, target, table, phases):
    smem = pl.BlockSpec(memory_space=pltpu.SMEM)
    anyw = pl.BlockSpec(memory_space=pl.ANY)
    vmem = pl.BlockSpec(memory_space=pltpu.VMEM)
    shapes = [
        ((512, 1024), BF), ((822, 512), F32), ((128, 512), F32), ((RELK, 512), BF), ((RELK, 512), BF),
        ((RELK, 512), BF), ((256, 512), BF), ((256, RELK), BF), ((256, 1024), BF),
        ((256, 512), F32), ((256, 512), F32), ((256, 512), F32), ((256, 512), F32),
        ((2, 128, 1024), BF), ((2, 64, 1024), BF), ((2, 64, 1024), BF), ((4, 64, 256), BF),
        ((4, 16, 1024), BF), ((64, 256), BF), ((16, 1024), BF), ((4, 16, 256), BF),
        ((4, 16, 256), BF), ((8, 2, 16, 256), BF), ((2, 2, 128, 1024), BF),
        ((512, 256), F32), ((512, 256), BF), ((256, 512), BF), ((512, 128), F32),
        ((256, 512), BF), ((256, 512), BF), ((RELP, 256), BF),
        ((256, 1024), BF), ((256, 1024), F32), ((256, 1024), BF),
        ((RELP, 256), BF), ((RELP, 256), F32), ((RELP, 256), BF),
        ((256, 1024), BF), ((RELP, 256), BF), ((3, 256, 256), BF), ((3, RY, 256), BF),
        ((256, 256), F32), ((256, 256), F32), ((256, 256), BF), ((256, 256), BF),
        ((3, 64, 256), BF), ((3, 64, 256), BF), ((64, 256), F32), ((64, 256), F32),
        ((64, 256), BF), ((64, 256), BF), ((7, 16, 128), BF), ((7, 16, 128), BF),
    ]
    return pl.pallas_call(
        step_kernel,
        out_shape=(
            jax.ShapeDtypeStruct((1, 256), F32),
            jax.ShapeDtypeStruct((256, 1024), BF),
            jax.ShapeDtypeStruct((512, 1024), BF),
            jax.ShapeDtypeStruct((4, 256, 512), BF),
        ),
        in_specs=[smem, smem, vmem, vmem, vmem, anyw, anyw],
        out_specs=(vmem, vmem, vmem, vmem),
        scratch_shapes=[pltpu.VMEM(shape, kind) for shape, kind in shapes]
        + [
            pltpu.SemaphoreType.DMA((N_COPY,)),
            pltpu.SemaphoreType.DMA((N_COPY,)),
            pltpu.SemaphoreType.DMA((2,)),
        ],
        compiler_params=pltpu.CompilerParams(collective_id=0, has_side_effects=True),
    )(owner, local, head, rel, target, table, phases)


def finish_kernel(owner_s, local_s, me_s, loss, head, ga, gb, loss_o, head_o, table_o, rel_o):
    loss_o[...] = loss[...]
    head_o[...] = head[...]
    for n in range(4):
        table_o[pl.ds(n * BLK, BLK), :] = jnp.zeros((BLK, 1024), BF)
        hits = [(owner_s[b] == me_s[0]) & (local_s[b] == n) for b in range(4)]

        @pl.when(hits[0] | hits[1] | hits[2] | hits[3])
        def _():
            total = jnp.zeros((BLK, 1024), F32)
            for b in range(4):
                total = total + ga[pl.ds(b * BLK, BLK), :].astype(F32) * hits[b].astype(F32)
            table_o[pl.ds(n * BLK, BLK), :] = total.astype(BF)

    for k in range(3):
        rel_o[pl.ds(k * RY, RY), :] = gb[k, pl.ds(0, RY), :].astype(F32)
    rel_o[pl.ds(3 * RY, 822 - 3 * RY), :] = gb[3, pl.ds(0, 822 - 3 * RY), :].astype(F32)


def finish(owner, local, entity, loss, head, ga, gb):
    smem = pl.BlockSpec(memory_space=pltpu.SMEM)
    vmem = pl.BlockSpec(memory_space=pltpu.VMEM)
    return pl.pallas_call(
        finish_kernel,
        out_shape=(
            jax.ShapeDtypeStruct((1, 256), F32),
            jax.ShapeDtypeStruct((256, 1024), BF),
            jax.ShapeDtypeStruct((512, 1024), BF),
            jax.ShapeDtypeStruct((822, 512), F32),
        ),
        in_specs=[smem, smem, smem, vmem, vmem, vmem, vmem],
        out_specs=(vmem, vmem, vmem, vmem),
    )(owner, local, entity, loss, head, ga, gb)


def body(entity_table, rel_phases, head_ids, rel_ids, target_pos, block_owner, block_local):
    rows = [ids.reshape(1, 256) for ids in (head_ids, rel_ids, target_pos)]
    loss, head, ga, gb = step(block_owner, block_local, *rows, entity_table, rel_phases)
    entity = lax.axis_index(ENT).astype(jnp.int32).reshape(1)
    loss, head, table, rel = finish(block_owner, block_local, entity, loss, head, ga, gb)
    return loss.reshape(256), head, table, rel


def solution(mesh):
    finer = Mesh(mesh.devices.reshape(4, 4, 4, 2, mesh.shape["grp"]), ENT_GRP)
    placed = (P(ENT, None), P(), P(ENT_GRP), P(ENT_GRP), P(ENT_GRP), P(), P())
    return jax.shard_map(
        body,
        mesh=finer,
        in_specs=placed,
        out_specs=(P(ENT_GRP), P(ENT_GRP, None), P(ENT, None), P()),
        check_vma=False,
    )
```

time: 117 us -> 80.7 us (0.69)
  other arithmetic: 24.9 us -> 0 us
  local copies, waits for them, and re-layouts: 6.55 us -> 0 us
  matrix products: 5.01 us -> 0 us
    another operation x2 -> x0, other arithmetic: 6.2 us -> none
    gather x3 -> x0, local copies, waits for them, and re-layouts: 5.28 us -> none  [the longest x1 2.35 us: body(): jnp.take_along_axis(logit_scores, target_pos[:, None], axis=1)[:, 0]]
    convert_element_type x4 -> x0, other arithmetic: 5.07 us -> none  [the longest x1 2.65 us: body(): rel_grad = rel_sum.reshape(RELP, half_dim)[:rel_count].astype(F32)]
    dot_general x3 -> x0, matrix products: 5.01 us -> none  [the longest x1 2.53 us: body(): lax.dot_general(weights_reduced_precision, query_reduced_precision, (((0,...]
    reduce_sum x4 -> x0, other arithmetic: 3.72 us -> none  [the longest x1 1.8 us: body(): placed = jnp.sum(jnp.where(selector[:, :, None, None], blocks, 0.0), axis=0)]
    scatter-add x1 -> x0, other arithmetic: 3.57 us -> none  [body(): rel_part = jax.ops.segment_sum(angle_grad, rel_ids, num_segments=RELP)]
    and x3 -> x0, other arithmetic: 2.1 us -> none  [the longest x1 0.73 us: body(): (block_owner == lax.axis_index(ENT))[:, None]]
    select_n x3 -> x0, other arithmetic: 2.04 us -> none  [the longest x1 0.68 us: body(): heads = jnp.take(entity_table, head_ids, axis=0).astype(jnp.float32)]
where the time goes in v2:
time: 80.7 us; the launch traced here: 80.5 us
  Pallas kernels  79.9 us (99%)
    pallas_call x1, Pallas kernels, step(): pl.pallas_call(step_kernel, out_shape=(jax.ShapeDtypeStruct((1, 256), F32...  76.4 us
    pallas_call x1, Pallas kernels, finish(): pl.pallas_call(finish_kernel, out_shape=(jax.ShapeDtypeStruct((1, 256), F...  3.53 us

profile of v2, /device:TPU:1, one launch (start us, length us, event | category | flops | bytes accessed | tf_op | source)
XLA Modules:
  0.0 80.5 jit_solution(14070829061229985948)
XLA Ops:
  0.6 76.4 %shard_map.102 = (f32[1,256]{1,0:T(1,128)}, bf16[256,1024]{1,0:T(8,128)(2,1)}, bf16[512,1024]{1,0:T(8,128)(2,1)}, bf16[4,256,512]{2,1,0:T(8,128)(2,1)}) custom-call(s32[4]{0:T(128)} %owner_s.3, s32[4]{0:T(128)} %local_s.3, s32[1,256]{1,0:T(1,128)} %bitcast.5, s32[1,256]{1,0:T(1,128)} %bitcast.6, s32[1,256]{1,0:T(1,128)} %bitcast.7, ...), custom_call_target="tpu_custom_call" | custom-call | tf_op jit(solution)/shard_map/pallas_call | solution.py:461
  77.0 3.5 %shard_map.103 = (f32[1,256]{1,0:T(1,128)}, bf16[256,1024]{1,0:T(8,128)(2,1)}, bf16[512,1024]{1,0:T(8,128)(2,1)}, f32[822,512]{1,0:T(8,128)}) custom-call(s32[4]{0:T(128)} %owner_s.3, s32[4]{0:T(128)} %local_s.3, s32[1]{0:T(128)} %bitcast.me_s, f32[1,256]{1,0:T(1,128)} %get-tuple-element.12.loss, bf16[256,1024]{1,0:T(8,128)(2,1)} %get-tuple-element.13.head, ...), custom_call_target="tpu_custom_call" | custom-call | tf_op jit(solution)/shard_map/pallas_call | solution.py:503
